TPU v7x, 32 devices: a whole 2x2x4 slice. The times are simulated.
32 devices in a mesh: tm: 8 (over z, x), mp: 4 (over y, core).
Axes of the slice: x: 2, y: 2, z: 4, core: 2. Of those that a mesh axis runs over, the one named last changes fastest.
Arguments:
- features: bfloat16 [256, 2048], P('tm'), may hold values from -6 to 6
- w_in: bfloat16 [2048, 4096], P(None, 'mp'), may hold values from -0.125 to 0.125
- b_in: float32 [4096], P('mp'), may hold values from -5 to 5
- output_weight: bfloat16 [4096, 256], P('mp'), may hold values from -0.09375 to 0.09375
- final_offset_entries: float32 [256], replicated, may hold values from -3 to 3
- transition: float32 [256, 256], replicated, may hold values from -1 to 1
- gains: float32 [256, 256], P('tm'), may hold values from 0 to 1
- smooth_gains: float32 [256, 256], P('tm'), may hold values from 0 to 1
Outputs:
- filtered: float32 [256, 256], P(('tm', 'mp'))
- smoothed: float32 [256, 256], P(('tm', 'mp'))
All inputs are finite; a program needn't handle non-finite values.
Results may differ from a plain program's by a relative error of at most 0.0021.
Values sent between devices are 32-bit elements; how exact they have to be, the bound alone decides.
A program may use at most 128 MiB of HBM per device.

v0:
```python
import jax
import jax.numpy as jnp
from jax import lax
from jax.sharding import PartitionSpec as P

HIGH = lax.Precision.HIGHEST


def passed_along(value, axis, steps):
    count = lax.axis_size(axis)
    initial, last = (max(0, -steps), min(count, count - steps))
    return lax.ppermute(value, axis, [(source, source + steps) for source in range(initial, last)])


def compose_diagonal(earlier, later):
    return (later[0] * earlier[0], later[0] * earlier[1] + later[1])


def sweep_up(mats, vecs):
    levels = [(mats, vecs)]
    while mats.shape[0] > 1:
        count = mats.shape[0]
        half = count // 2
        first_m = mats[0 : 2 * half : 2]
        second_m = mats[1 : 2 * half : 2]
        first_v = vecs[0 : 2 * half : 2]
        second_v = vecs[1 : 2 * half : 2]
        new_m = jnp.einsum("bij,bjk->bik", second_m, first_m, precision=HIGH)
        new_v = jnp.einsum("bij,bj->bi", second_m, first_v, precision=HIGH) + second_v
        mats, vecs = (new_m, new_v)
        levels.append((mats, vecs))
    return levels


def sweep_down(levels, incoming):
    states = incoming[None]
    for level in range(len(levels) - 2, -1, -1):
        mats, vecs = levels[level]
        count = mats.shape[0]
        half = count // 2
        evens = states
        odds = (
            jnp.einsum("bij,bj->bi", mats[0 : 2 * half : 2], evens, precision=HIGH)
            + vecs[0 : 2 * half : 2]
        )
        paired = jnp.stack([evens, odds], 1).reshape(2 * half, states.shape[1])
        states = paired
    return states


def carry_forward(block_m, block_v):
    grid = block_v.shape[0]

    def relay_time(step, incoming):
        outgoing = jnp.dot(block_m, incoming, precision=HIGH) + block_v
        return passed_along(outgoing, "tm", 1)

    return lax.fori_loop(0, lax.axis_size("tm") - 1, relay_time, jnp.zeros((grid,), jnp.float32))


def carry_backward(block_d, block_v):
    grid = block_v.shape[0]

    def relay_time(step, incoming):
        outgoing = block_d * incoming + block_v
        return passed_along(outgoing, "tm", -1)

    return lax.fori_loop(0, lax.axis_size("tm") - 1, relay_time, jnp.zeros((grid,), jnp.float32))


def on_device(
    features, w_in, b_in, output_weight, final_offset_entries, transition, gains, smooth_gains
):
    pre = jnp.dot(features, w_in, preferred_element_type=jnp.float32) + b_in
    hidden_layer = jax.nn.gelu(pre, approximate=True).astype(jnp.bfloat16)
    partial_measurement = jnp.dot(hidden_layer, output_weight, preferred_element_type=jnp.float32)
    share = features.shape[0] // lax.axis_size("mp")
    mp_place = lax.axis_index("mp")
    time_last = lax.axis_index("tm") == lax.axis_size("tm") - 1
    measured_values = lax.psum(partial_measurement, "mp") + final_offset_entries
    weight_here = smooth_gains
    forward_m = (1.0 - gains)[:, :, None] * transition[None]
    forward_variance = gains * measured_values
    levels = sweep_up(forward_m, forward_variance)
    incoming = carry_forward(levels[-1][0][0], levels[-1][1][0])
    before = sweep_down(levels, incoming)
    filtered = jnp.einsum("tij,tj->ti", forward_m, before, precision=HIGH) + forward_variance
    closing = jnp.where(time_last, 0.0, 1.0).astype(jnp.float32)
    weight_here = weight_here.at[-1].multiply(closing)
    predicted = jnp.dot(filtered, transition.T, precision=HIGH)
    backward_d = weight_here[::-1]
    backward_v = (filtered - weight_here * predicted)[::-1]
    prefix_d, prefix_v = lax.associative_scan(compose_diagonal, (backward_d, backward_v), axis=0)
    later_state = carry_backward(prefix_d[-1], prefix_v[-1])
    smoothed = (prefix_d * later_state[None] + prefix_v)[::-1]
    filtered = lax.dynamic_slice_in_dim(filtered, mp_place * share, share, 0)
    smoothed = lax.dynamic_slice_in_dim(smoothed, mp_place * share, share, 0)
    return (filtered, smoothed)


def solution(mesh):
    placed = (
        P("tm", None),
        P(None, "mp"),
        P("mp"),
        P("mp", None),
        P(),
        P(),
        P("tm", None),
        P("tm", None),
    )
    return jax.shard_map(
        on_device,
        mesh=mesh,
        in_specs=placed,
        out_specs=(P(("tm", "mp"), None), P(("tm", "mp"), None)),
        check_vma=False,
    )
```

profile of v0, /device:TPU:0, one launch (start us, length us, event | category | flops | bytes accessed | tf_op | source)
XLA Modules:
  0.0 162.2 jit_solution(11965233251702824456)
XLA Ops:
  0.7 0.8 copy.85
  1.7 3.2 %fusion.40 = f32[32,256]{1,0:T(8,128)S(1)} fusion(bf16[1024,256]{1,0:T(8,128)(2,1)S(1)} %copy-done, bf16[32,2048]{1,0:T(8,128)(2,1)} %param.14, bf16[2048,1024]{1,0:T(8,128)(2,1)} %param.15, f32[1024]{0:T(1024)} %param.16), kind=kOutput, calls=%fused_computation.49 | convolution fusion | flops 151322624 | bytes 4886528 | tf_op jit(solution)/shard_map/dot_general | solution.py:76
  4.9 12.9 %psum.7 = f32[32,256]{1,0:T(8,128)S(1)} all-reduce(f32[32,256]{1,0:T(8,128)S(1)} %fusion.40), channel_id=1, replica_groups=mesh['tm'=8,'mp'=4] {'mp'}, use_global_device_ids=true, to_apply=%region_0.0 | all-reduce | flops 8192 | bytes 65536 | tf_op jit(solution)/shard_map/psum | solution.py:80
  17.9 3.9 %broadcast_multiply_fusion = f32[32,256,256]{2,1,0:T(8,128)} fusion(f32[256,256]{1,0:T(8,128)S(1)} %copy-done.3, f32[32,256]{1,0:T(8,128)S(1)} %get-tuple-element.76), kind=kLoop, calls=%fused_computation.1 | loop fusion | flops 2097152 | bytes 8683520 | tf_op jit(solution)/shard_map/mul | solution.py:82
  21.8 5.8 %fusion.4 = f32[16,1,256]{2,1,0:T(1,128)S(1)} fusion(f32[32,256,256]{2,1,0:T(8,128)} %broadcast_multiply_fusion, f32[16,256,1]{1,0,2:T(8,128)S(1)} %bitcast.86), kind=kOutput, calls=%fused_computation.6 | convolution fusion | flops 12582912 | bytes 4227072 | tf_op jit(solution)/shard_map/bij,bj->bi/dot_general | solution.py:29
  27.6 8.5 %fusion.2 = f32[16,256,256]{2,1,0:T(8,128)S(1)} fusion(f32[32,256,256]{2,1,0:T(8,128)} %broadcast_multiply_fusion), kind=kOutput, calls=%fused_computation.4 | convolution fusion | flops 3221225472 | bytes 12582912 | tf_op jit(solution)/shard_map/bij,bjk->bik/dot_general | solution.py:28
  36.1 2.0 %copy-done.1 = f32[16,256,256]{2,1,0:T(8,128)} copy-done((f32[16,256,256]{2,1,0:T(8,128)}, f32[16,256,256]{2,1,0:T(8,128)S(1)}, u32[]{:S(2)}) %copy-start.1) | copy-done | bytes 4194328
  38.1 1.8 %fusion.12 = f32[8,1,256]{2,1,0:T(1,128)S(1)} fusion(f32[16,256,256]{2,1,0:T(8,128)S(1)} %fusion.2, f32[8,256,1]{1,0,2:T(8,128)S(1)} %bitcast.88), kind=kOutput, calls=%fused_computation.14 | convolution fusion | flops 6291456 | bytes 2113536 | tf_op jit(solution)/shard_map/bij,bj->bi/dot_general | solution.py:29
  40.0 4.3 %fusion.10 = f32[8,256,256]{2,1,0:T(8,128)S(1)} fusion(f32[16,256,256]{2,1,0:T(8,128)} %copy-done.1), kind=kOutput, calls=%fused_computation.12 | convolution fusion | flops 1610612736 | bytes 6291456 | tf_op jit(solution)/shard_map/bij,bjk->bik/dot_general | solution.py:28
  44.3 1.0 fusion.21
  45.3 1.2 fusion.19
  46.5 1.0 copy-done.2
  48.1 1.9 %fusion.26 = f32[2,256,256]{2,1,0:T(8,128)S(1)} fusion(f32[4,256,256]{2,1,0:T(8,128)} %copy-done.2), kind=kOutput, calls=%fused_computation.32 | convolution fusion | flops 402653184 | bytes 1572864 | tf_op jit(solution)/shard_map/bij,bjk->bik/dot_general | solution.py:28
  50.7 43.5 %while.21 = (s32[]{:T(128)}, f32[256]{0:T(256)S(1)}, f32[256,256]{1,0:T(8,128)S(1)}, f32[256]{0:T(256)S(1)}, s32[]{:T(128)}) while((s32[]{:T(128)}, f32[256]{0:T(256)S(1)}, f32[256,256]{1,0:T(8,128)S(1)}, f32[256]{0:T(256)S(1)}, s32[]{:T(128)}) %tuple.61), condition=%wide.region_2.0_spmd, body=%wide.region_1.0_spmd.sunk | while | flops 786690 | bytes 271461 | solution.py:58
  51.0 3.4 %collective-permute-start = (f32[256]{0:T(256)S(1)}, f32[256]{0:T(256)S(1)}, u32[]{:S(2)}, u32[]{:S(2)}) collective-permute-start(f32[256]{0:T(256)S(1)} %add.331), channel_id=1, source_target_pairs={{0,4},{4,8},{8,12},{12,16},{16,20},{20,24},{24,28},{1,5},{5,9},{9,... | collective-permute-start | bytes 3080 | tf_op jit(solution)/shard_map/while/body/eval_jaxpr/ppermute | solution.py:12
  54.4 1.3 collective-permute-done
  56.0 4.2 %collective-permute-start = (f32[256]{0:T(256)S(1)}, f32[256]{0:T(256)S(1)}, u32[]{:S(2)}, u32[]{:S(2)}) collective-permute-start(f32[256]{0:T(256)S(1)} %add.331), channel_id=1, source_target_pairs={{0,4},{4,8},{8,12},{12,16},{16,20},{20,24},{24,28},{1,5},{5,9},{9,... | collective-permute-start | bytes 3080 | tf_op jit(solution)/shard_map/while/body/eval_jaxpr/ppermute | solution.py:12
  60.2 1.3 collective-permute-done
  61.8 4.4 %collective-permute-start = (f32[256]{0:T(256)S(1)}, f32[256]{0:T(256)S(1)}, u32[]{:S(2)}, u32[]{:S(2)}) collective-permute-start(f32[256]{0:T(256)S(1)} %add.331), channel_id=1, source_target_pairs={{0,4},{4,8},{8,12},{12,16},{16,20},{20,24},{24,28},{1,5},{5,9},{9,... | collective-permute-start | bytes 3080 | tf_op jit(solution)/shard_map/while/body/eval_jaxpr/ppermute | solution.py:12
  66.2 1.3 collective-permute-done
  67.7 5.1 %collective-permute-start = (f32[256]{0:T(256)S(1)}, f32[256]{0:T(256)S(1)}, u32[]{:S(2)}, u32[]{:S(2)}) collective-permute-start(f32[256]{0:T(256)S(1)} %add.331), channel_id=1, source_target_pairs={{0,4},{4,8},{8,12},{12,16},{16,20},{20,24},{24,28},{1,5},{5,9},{9,... | collective-permute-start | bytes 3080 | tf_op jit(solution)/shard_map/while/body/eval_jaxpr/ppermute | solution.py:12
  72.9 1.3 collective-permute-done
  74.4 5.1 %collective-permute-start = (f32[256]{0:T(256)S(1)}, f32[256]{0:T(256)S(1)}, u32[]{:S(2)}, u32[]{:S(2)}) collective-permute-start(f32[256]{0:T(256)S(1)} %add.331), channel_id=1, source_target_pairs={{0,4},{4,8},{8,12},{12,16},{16,20},{20,24},{24,28},{1,5},{5,9},{9,... | collective-permute-start | bytes 3080 | tf_op jit(solution)/shard_map/while/body/eval_jaxpr/ppermute | solution.py:12
  79.6 1.3 collective-permute-done
  81.1 5.1 %collective-permute-start = (f32[256]{0:T(256)S(1)}, f32[256]{0:T(256)S(1)}, u32[]{:S(2)}, u32[]{:S(2)}) collective-permute-start(f32[256]{0:T(256)S(1)} %add.331), channel_id=1, source_target_pairs={{0,4},{4,8},{8,12},{12,16},{16,20},{20,24},{24,28},{1,5},{5,9},{9,... | collective-permute-start | bytes 3080 | tf_op jit(solution)/shard_map/while/body/eval_jaxpr/ppermute | solution.py:12
  86.3 1.3 collective-permute-done
  87.8 5.1 %collective-permute-start = (f32[256]{0:T(256)S(1)}, f32[256]{0:T(256)S(1)}, u32[]{:S(2)}, u32[]{:S(2)}) collective-permute-start(f32[256]{0:T(256)S(1)} %add.331), channel_id=1, source_target_pairs={{0,4},{4,8},{8,12},{12,16},{16,20},{20,24},{24,28},{1,5},{5,9},{9,... | collective-permute-start | bytes 3080 | tf_op jit(solution)/shard_map/while/body/eval_jaxpr/ppermute | solution.py:12
  93.0 1.3 collective-permute-done
  94.6 1.6 %fusion.24 = f32[2,1,256]{2,1,0:T(1,128)S(1)} fusion(f32[4,256,256]{2,1,0:T(8,128)} %copy-done.2, f32[2,256,1]{1,0,2:T(2,128)S(1)} %get-tuple-element.101), kind=kOutput, calls=%fused_computation.30 | convolution fusion | flops 1572864 | bytes 528384 | tf_op jit(solution)/shard_map/bij,bj->bi/dot_general | solution.py:43
  96.3 1.0 fusion.17
  97.3 3.4 %fusion.8 = f32[8,1,256]{2,1,0:T(1,128)S(1)} fusion(f32[8,256,1]{1,2,0:T(1,128)S(1)} %reshape.98, f32[16,256,256]{2,1,0:T(8,128)} %copy-done.1), kind=kOutput, calls=%fused_computation.10 | convolution fusion | flops 6291456 | bytes 2113536 | tf_op jit(solution)/shard_map/bij,bj->bi/dot_general | solution.py:43
  100.9 5.8 %fusion = f32[16,1,256]{2,1,0:T(1,128)S(1)} fusion(f32[16,256,1]{1,2,0:T(1,128)S(1)} %reshape.100, f32[32,256,256]{2,1,0:T(8,128)} %broadcast_multiply_fusion), kind=kOutput, calls=%fused_computation.2 | convolution fusion | flops 12582912 | bytes 4227072 | tf_op jit(solution)/shard_map/bij,bj->bi/dot_general | solution.py:43
  106.8 7.6 %fusion.7 = f32[32,1,256]{2,1,0:T(1,128)S(1)} fusion(f32[32,256,1]{1,2,0:T(1,128)S(1)} %reshape.102, f32[256,256]{1,0:T(8,128)S(1)} %copy-done.4, f32[32,256]{1,0:T(8,128)S(1)} %get-tuple-element.76), kind=kOutput, calls=%fused_computation.9 | convolution fusion | flops 27262976 | bytes 360448 | tf_op jit(solution)/shard_map/tij,tj->ti/dot_general | solution.py:87
  116.4 45.1 %while.22 = (s32[]{:T(128)}, f32[256]{0:T(256)S(1)}, f32[256]{0:T(256)S(1)}, f32[256]{0:T(256)S(1)}, s32[]{:T(128)}) while((s32[]{:T(128)}, f32[256]{0:T(256)S(1)}, f32[256]{0:T(256)S(1)}, f32[256]{0:T(256)S(1)}, s32[]{:T(128)}) %tuple.63), condition=%wide.region_4.5_spmd, body=%wide.region_3.4_spmd.sunk | while | flops 514 | bytes 8293 | solution.py:68
  116.4 1.3 collective-permute-start.1
  117.7 5.3 %collective-permute-done.1 = f32[256]{0:T(256)S(1)} collective-permute-done((f32[256]{0:T(256)S(1)}, f32[256]{0:T(256)S(1)}, u32[]{:S(2)}, u32[]{:S(2)}) %collective-permute-start.1) | collective-permute-done | bytes 1056 | tf_op jit(solution)/shard_map/while/body/eval_jaxpr/ppermute | solution.py:12
  123.0 1.3 collective-permute-start.1
  124.3 5.3 %collective-permute-done.1 = f32[256]{0:T(256)S(1)} collective-permute-done((f32[256]{0:T(256)S(1)}, f32[256]{0:T(256)S(1)}, u32[]{:S(2)}, u32[]{:S(2)}) %collective-permute-start.1) | collective-permute-done | bytes 1056 | tf_op jit(solution)/shard_map/while/body/eval_jaxpr/ppermute | solution.py:12
  129.7 1.3 collective-permute-start.1
  131.0 5.1 %collective-permute-done.1 = f32[256]{0:T(256)S(1)} collective-permute-done((f32[256]{0:T(256)S(1)}, f32[256]{0:T(256)S(1)}, u32[]{:S(2)}, u32[]{:S(2)}) %collective-permute-start.1) | collective-permute-done | bytes 1056 | tf_op jit(solution)/shard_map/while/body/eval_jaxpr/ppermute | solution.py:12
  136.0 1.3 collective-permute-start.1
  137.3 5.1 %collective-permute-done.1 = f32[256]{0:T(256)S(1)} collective-permute-done((f32[256]{0:T(256)S(1)}, f32[256]{0:T(256)S(1)}, u32[]{:S(2)}, u32[]{:S(2)}) %collective-permute-start.1) | collective-permute-done | bytes 1056 | tf_op jit(solution)/shard_map/while/body/eval_jaxpr/ppermute | solution.py:12
  142.4 1.3 collective-permute-start.1
  143.7 5.1 %collective-permute-done.1 = f32[256]{0:T(256)S(1)} collective-permute-done((f32[256]{0:T(256)S(1)}, f32[256]{0:T(256)S(1)}, u32[]{:S(2)}, u32[]{:S(2)}) %collective-permute-start.1) | collective-permute-done | bytes 1056 | tf_op jit(solution)/shard_map/while/body/eval_jaxpr/ppermute | solution.py:12
  148.7 1.3 collective-permute-start.1
  150.0 5.1 %collective-permute-done.1 = f32[256]{0:T(256)S(1)} collective-permute-done((f32[256]{0:T(256)S(1)}, f32[256]{0:T(256)S(1)}, u32[]{:S(2)}, u32[]{:S(2)}) %collective-permute-start.1) | collective-permute-done | bytes 1056 | tf_op jit(solution)/shard_map/while/body/eval_jaxpr/ppermute | solution.py:12
  155.1 1.3 collective-permute-start.1
  156.4 5.1 %collective-permute-done.1 = f32[256]{0:T(256)S(1)} collective-permute-done((f32[256]{0:T(256)S(1)}, f32[256]{0:T(256)S(1)}, u32[]{:S(2)}, u32[]{:S(2)}) %collective-permute-start.1) | collective-permute-done | bytes 1056 | tf_op jit(solution)/shard_map/while/body/eval_jaxpr/ppermute | solution.py:12
  (155 shorter events, 6.5 us)
Async XLA Ops:
  0.6 1.1 copy-start
  0.6 17.2 %copy-start.6 = (f32[256]{0:T(256)S(1)}, f32[256]{0:T(256)}, u32[]{:S(2)}) copy-start(f32[256]{0:T(256)} %param.18) | copy-start | bytes 3076
  0.7 17.2 %copy-start.5 = (f32[32,256]{1,0:T(8,128)S(1)}, f32[32,256]{1,0:T(8,128)}, u32[]{:S(2)}) copy-start(f32[32,256]{1,0:T(8,128)} %param.20) | copy-start | bytes 98308
  0.7 17.2 %copy-start.3 = (f32[256,256]{1,0:T(8,128)S(1)}, f32[256,256]{1,0:T(8,128)}, u32[]{:S(2)}) copy-start(f32[256,256]{1,0:T(8,128)} %param.19) | copy-start | bytes 786436
  36.1 2.0 %copy-start.1 = (f32[16,256,256]{2,1,0:T(8,128)}, f32[16,256,256]{2,1,0:T(8,128)S(1)}, u32[]{:S(2)}) copy-start(f32[16,256,256]{2,1,0:T(8,128)S(1)} %fusion.2) | copy-start | bytes 12582916
  46.5 1.0 copy-start.2
  51.0 4.7 %collective-permute-start = (f32[256]{0:T(256)S(1)}, f32[256]{0:T(256)S(1)}, u32[]{:S(2)}, u32[]{:S(2)}) collective-permute-start(f32[256]{0:T(256)S(1)} %add.331), channel_id=1, source_target_pairs={{0,4},{4,8},{8,12},{12,16},{16,20},{20,24},{24,28},{1,5},{5,9},{9,... | collective-permute-start | bytes 3080 | tf_op jit(solution)/shard_map/while/body/eval_jaxpr/ppermute | solution.py:12
  56.0 5.5 %collective-permute-start = (f32[256]{0:T(256)S(1)}, f32[256]{0:T(256)S(1)}, u32[]{:S(2)}, u32[]{:S(2)}) collective-permute-start(f32[256]{0:T(256)S(1)} %add.331), channel_id=1, source_target_pairs={{0,4},{4,8},{8,12},{12,16},{16,20},{20,24},{24,28},{1,5},{5,9},{9,... | collective-permute-start | bytes 3080 | tf_op jit(solution)/shard_map/while/body/eval_jaxpr/ppermute | solution.py:12
  61.8 5.7 %collective-permute-start = (f32[256]{0:T(256)S(1)}, f32[256]{0:T(256)S(1)}, u32[]{:S(2)}, u32[]{:S(2)}) collective-permute-start(f32[256]{0:T(256)S(1)} %add.331), channel_id=1, source_target_pairs={{0,4},{4,8},{8,12},{12,16},{16,20},{20,24},{24,28},{1,5},{5,9},{9,... | collective-permute-start | bytes 3080 | tf_op jit(solution)/shard_map/while/body/eval_jaxpr/ppermute | solution.py:12
  67.7 6.4 %collective-permute-start = (f32[256]{0:T(256)S(1)}, f32[256]{0:T(256)S(1)}, u32[]{:S(2)}, u32[]{:S(2)}) collective-permute-start(f32[256]{0:T(256)S(1)} %add.331), channel_id=1, source_target_pairs={{0,4},{4,8},{8,12},{12,16},{16,20},{20,24},{24,28},{1,5},{5,9},{9,... | collective-permute-start | bytes 3080 | tf_op jit(solution)/shard_map/while/body/eval_jaxpr/ppermute | solution.py:12
  74.4 6.4 %collective-permute-start = (f32[256]{0:T(256)S(1)}, f32[256]{0:T(256)S(1)}, u32[]{:S(2)}, u32[]{:S(2)}) collective-permute-start(f32[256]{0:T(256)S(1)} %add.331), channel_id=1, source_target_pairs={{0,4},{4,8},{8,12},{12,16},{16,20},{20,24},{24,28},{1,5},{5,9},{9,... | collective-permute-start | bytes 3080 | tf_op jit(solution)/shard_map/while/body/eval_jaxpr/ppermute | solution.py:12
  81.1 6.4 %collective-permute-start = (f32[256]{0:T(256)S(1)}, f32[256]{0:T(256)S(1)}, u32[]{:S(2)}, u32[]{:S(2)}) collective-permute-start(f32[256]{0:T(256)S(1)} %add.331), channel_id=1, source_target_pairs={{0,4},{4,8},{8,12},{12,16},{16,20},{20,24},{24,28},{1,5},{5,9},{9,... | collective-permute-start | bytes 3080 | tf_op jit(solution)/shard_map/while/body/eval_jaxpr/ppermute | solution.py:12
  87.8 6.4 %collective-permute-start = (f32[256]{0:T(256)S(1)}, f32[256]{0:T(256)S(1)}, u32[]{:S(2)}, u32[]{:S(2)}) collective-permute-start(f32[256]{0:T(256)S(1)} %add.331), channel_id=1, source_target_pairs={{0,4},{4,8},{8,12},{12,16},{16,20},{20,24},{24,28},{1,5},{5,9},{9,... | collective-permute-start | bytes 3080 | tf_op jit(solution)/shard_map/while/body/eval_jaxpr/ppermute | solution.py:12
  94.6 12.2 %copy-start.4 = (f32[256,256]{1,0:T(8,128)S(1)}, f32[256,256]{1,0:T(8,128)}, u32[]{:S(2)}) copy-start(f32[256,256]{1,0:T(8,128)} %param.19) | copy-start | bytes 786436
  116.4 6.6 %collective-permute-start.1 = (f32[256]{0:T(256)S(1)}, f32[256]{0:T(256)S(1)}, u32[]{:S(2)}, u32[]{:S(2)}) collective-permute-start(f32[256]{0:T(256)S(1)} %multiply_add_fusion.7), channel_id=1, source_target_pairs={{4,0},{8,4},{12,8},{16,12},{20,16},{24,20},{28,24},{5,1},{9,5},{13... | collective-permute-start | bytes 3080 | tf_op jit(solution)/shard_map/while/body/eval_jaxpr/ppermute | solution.py:12
  123.0 6.6 %collective-permute-start.1 = (f32[256]{0:T(256)S(1)}, f32[256]{0:T(256)S(1)}, u32[]{:S(2)}, u32[]{:S(2)}) collective-permute-start(f32[256]{0:T(256)S(1)} %multiply_add_fusion.7), channel_id=1, source_target_pairs={{4,0},{8,4},{12,8},{16,12},{20,16},{24,20},{28,24},{5,1},{9,5},{13... | collective-permute-start | bytes 3080 | tf_op jit(solution)/shard_map/while/body/eval_jaxpr/ppermute | solution.py:12
  129.7 6.4 %collective-permute-start.1 = (f32[256]{0:T(256)S(1)}, f32[256]{0:T(256)S(1)}, u32[]{:S(2)}, u32[]{:S(2)}) collective-permute-start(f32[256]{0:T(256)S(1)} %multiply_add_fusion.7), channel_id=1, source_target_pairs={{4,0},{8,4},{12,8},{16,12},{20,16},{24,20},{28,24},{5,1},{9,5},{13... | collective-permute-start | bytes 3080 | tf_op jit(solution)/shard_map/while/body/eval_jaxpr/ppermute | solution.py:12
  136.0 6.4 %collective-permute-start.1 = (f32[256]{0:T(256)S(1)}, f32[256]{0:T(256)S(1)}, u32[]{:S(2)}, u32[]{:S(2)}) collective-permute-start(f32[256]{0:T(256)S(1)} %multiply_add_fusion.7), channel_id=1, source_target_pairs={{4,0},{8,4},{12,8},{16,12},{20,16},{24,20},{28,24},{5,1},{9,5},{13... | collective-permute-start | bytes 3080 | tf_op jit(solution)/shard_map/while/body/eval_jaxpr/ppermute | solution.py:12
  142.4 6.4 %collective-permute-start.1 = (f32[256]{0:T(256)S(1)}, f32[256]{0:T(256)S(1)}, u32[]{:S(2)}, u32[]{:S(2)}) collective-permute-start(f32[256]{0:T(256)S(1)} %multiply_add_fusion.7), channel_id=1, source_target_pairs={{4,0},{8,4},{12,8},{16,12},{20,16},{24,20},{28,24},{5,1},{9,5},{13... | collective-permute-start | bytes 3080 | tf_op jit(solution)/shard_map/while/body/eval_jaxpr/ppermute | solution.py:12
  148.7 6.4 %collective-permute-start.1 = (f32[256]{0:T(256)S(1)}, f32[256]{0:T(256)S(1)}, u32[]{:S(2)}, u32[]{:S(2)}) collective-permute-start(f32[256]{0:T(256)S(1)} %multiply_add_fusion.7), channel_id=1, source_target_pairs={{4,0},{8,4},{12,8},{16,12},{20,16},{24,20},{28,24},{5,1},{9,5},{13... | collective-permute-start | bytes 3080 | tf_op jit(solution)/shard_map/while/body/eval_jaxpr/ppermute | solution.py:12
  155.1 6.4 %collective-permute-start.1 = (f32[256]{0:T(256)S(1)}, f32[256]{0:T(256)S(1)}, u32[]{:S(2)}, u32[]{:S(2)}) collective-permute-start(f32[256]{0:T(256)S(1)} %multiply_add_fusion.7), channel_id=1, source_target_pairs={{4,0},{8,4},{12,8},{16,12},{20,16},{24,20},{28,24},{5,1},{9,5},{13... | collective-permute-start | bytes 3080 | tf_op jit(solution)/shard_map/while/body/eval_jaxpr/ppermute | solution.py:12
where the time goes:
time: 163 us; the launch traced here: 162 us
  matrix products  50.8 us (31%)
  waiting for transfers between devices  44.9 us (28%)
  starting transfers between devices  41.5 us (25%)
  blocking collectives  12.9 us (8%)
  local copies, waits for them, and re-layouts  6.12 us (4%)
  other arithmetic  4.38 us (3%)
    ppermute x14, waiting for transfers between devices, passed_along(): lax.ppermute(value, axis, [(source, source + steps) for source in range(i...  44.9 us
    ppermute x14, starting transfers between devices, passed_along(): lax.ppermute(value, axis, [(source, source + steps) for source in range(i...  41.5 us
    dot_general x5, matrix products, sweep_up(): new_m = jnp.einsum('bij,bjk->bik', second_m, first_m, precision=HIGH)  16.2 us
    psum x1, blocking collectives, on_device(): measured_values = lax.psum(partial_measurement, 'mp') + final_offset_entries  12.9 us
    dot_general x5, matrix products, sweep_down(): jnp.einsum('bij,bj->bi', mats[0:2 * half:2], evens, precision=HIGH)  12.1 us
    dot_general x5, matrix products, sweep_up(): jnp.einsum('bij,bj->bi', second_m, first_v, precision=HIGH) + second_v  9.4 us
    dot_general x1, matrix products, on_device(): jnp.einsum('tij,tj->ti', forward_m, before, precision=HIGH)  7.61 us
    unnamed x15, local copies, waits for them, and re-layouts  4.02 us
  transfers between devices with their start and end apart: 14, of which 14 were waited for; matrix products, arithmetic and copies ran while one was open for 0% of the time, Pallas kernels for 0%

commit v1 on v0

--- a/solution.py
+++ b/solution.py
@@ -4,6 +4,11 @@
 from jax.sharding import PartitionSpec as P
 
 HIGH = lax.Precision.HIGHEST
+
+
+def connect_values(work_x):
+    fresh = lax.all_gather(work_x, "mp").sum(axis=0)
+    return fresh
 
 
 def passed_along(value, axis, steps):
@@ -77,7 +82,7 @@
     share = features.shape[0] // lax.axis_size("mp")
     mp_place = lax.axis_index("mp")
     time_last = lax.axis_index("tm") == lax.axis_size("tm") - 1
-    measured_values = lax.psum(partial_measurement, "mp") + final_offset_entries
+    measured_values = connect_values(partial_measurement) + final_offset_entries
     weight_here = smooth_gains
     forward_m = (1.0 - gains)[:, :, None] * transition[None]
     forward_variance = gains * measured_values

time: 163 us -> 157 us (0.963)
  blocking collectives: 12.9 us -> 6.53 us
    psum x1 -> x0, blocking collectives: 12.9 us -> none  [on_device(): measured_values = lax.psum(partial_measurement, 'mp') + final_offset_entries]
    all_gather x0 -> x1, blocking collectives: none -> 6.53 us  [connect_values(): fresh = lax.all_gather(work_x, 'mp').sum(axis=0)]
where the time goes in v1:
time: 157 us; the launch traced here: 156 us
  matrix products  50.8 us (32%)
  waiting for transfers between devices  44.9 us (29%)
  starting transfers between devices  41.9 us (27%)
  blocking collectives  6.53 us (4%)
  local copies, waits for them, and re-layouts  6.12 us (4%)
  other arithmetic  4.39 us (3%)
    ppermute x14, waiting for transfers between devices, passed_along(): lax.ppermute(value, axis, [(source, source + steps) for source in range(i...  44.9 us
    ppermute x14, starting transfers between devices, passed_along(): lax.ppermute(value, axis, [(source, source + steps) for source in range(i...  41.9 us
    dot_general x5, matrix products, sweep_up(): new_m = jnp.einsum('bij,bjk->bik', second_m, first_m, precision=HIGH)  16.2 us
    dot_general x5, matrix products, sweep_down(): jnp.einsum('bij,bj->bi', mats[0:2 * half:2], evens, precision=HIGH)  12.1 us
    dot_general x5, matrix products, sweep_up(): jnp.einsum('bij,bj->bi', second_m, first_v, precision=HIGH) + second_v  9.4 us
    dot_general x1, matrix products, on_device(): jnp.einsum('tij,tj->ti', forward_m, before, precision=HIGH)  7.61 us
    all_gather x1, blocking collectives, connect_values(): fresh = lax.all_gather(work_x, 'mp').sum(axis=0)  6.53 us
    unnamed x15, local copies, waits for them, and re-layouts  4.02 us
  transfers between devices with their start and end apart: 14, of which 14 were waited for; matrix products, arithmetic and copies ran while one was open for 0% of the time, Pallas kernels for 0%

profile of v1, /device:TPU:0, one launch (start us, length us, event | category | flops | bytes accessed | tf_op | source)
XLA Modules:
  0.0 156.1 jit_solution(7917590339276007904)
XLA Ops:
  0.7 0.8 copy.86
  1.7 3.2 %fusion.40 = f32[32,256]{1,0:T(8,128)S(1)} fusion(bf16[1024,256]{1,0:T(8,128)(2,1)S(1)} %copy-done, bf16[32,2048]{1,0:T(8,128)(2,1)} %param.14, bf16[2048,1024]{1,0:T(8,128)(2,1)} %param.15, f32[1024]{0:T(1024)} %param.16), kind=kOutput, calls=%fused_computation.49 | convolution fusion | flops 151322624 | bytes 4886528 | tf_op jit(solution)/shard_map/dot_general | solution.py:81
  4.9 6.5 %all-gather = f32[128,256]{1,0:T(8,128)S(1)} all-gather(f32[32,256]{1,0:T(8,128)S(1)} %fusion.40), channel_id=2, replica_groups=mesh['tm'=8,'mp'=4] {'mp'}, dimensions={0}, use_global_device_ids=true | all-gather | bytes 163840 | tf_op jit(solution)/shard_map/all_gather | solution.py:10
  11.5 3.9 %broadcast_multiply_fusion = f32[32,256,256]{2,1,0:T(8,128)} fusion(f32[256,256]{1,0:T(8,128)S(1)} %copy-done.3, f32[32,256]{1,0:T(8,128)S(1)} %get-tuple-element.76), kind=kLoop, calls=%fused_computation.1 | loop fusion | flops 2097152 | bytes 8683520 | tf_op jit(solution)/shard_map/mul | solution.py:87
  15.4 5.8 %fusion.4 = f32[16,1,256]{2,1,0:T(1,128)S(1)} fusion(f32[32,256,256]{2,1,0:T(8,128)} %broadcast_multiply_fusion, f32[16,256,1]{1,0,2:T(8,128)S(1)} %bitcast.88), kind=kOutput, calls=%fused_computation.6 | convolution fusion | flops 12582912 | bytes 4227072 | tf_op jit(solution)/shard_map/bij,bj->bi/dot_general | solution.py:34
  21.2 8.5 %fusion.2 = f32[16,256,256]{2,1,0:T(8,128)S(1)} fusion(f32[32,256,256]{2,1,0:T(8,128)} %broadcast_multiply_fusion), kind=kOutput, calls=%fused_computation.4 | convolution fusion | flops 3221225472 | bytes 12582912 | tf_op jit(solution)/shard_map/bij,bjk->bik/dot_general | solution.py:33
  29.7 2.0 %copy-done.1 = f32[16,256,256]{2,1,0:T(8,128)} copy-done((f32[16,256,256]{2,1,0:T(8,128)}, f32[16,256,256]{2,1,0:T(8,128)S(1)}, u32[]{:S(2)}) %copy-start.1) | copy-done | bytes 4194328
  31.7 1.8 %fusion.12 = f32[8,1,256]{2,1,0:T(1,128)S(1)} fusion(f32[16,256,256]{2,1,0:T(8,128)S(1)} %fusion.2, f32[8,256,1]{1,0,2:T(8,128)S(1)} %bitcast.90), kind=kOutput, calls=%fused_computation.14 | convolution fusion | flops 6291456 | bytes 2113536 | tf_op jit(solution)/shard_map/bij,bj->bi/dot_general | solution.py:34
  33.6 4.3 %fusion.10 = f32[8,256,256]{2,1,0:T(8,128)S(1)} fusion(f32[16,256,256]{2,1,0:T(8,128)} %copy-done.1), kind=kOutput, calls=%fused_computation.12 | convolution fusion | flops 1610612736 | bytes 6291456 | tf_op jit(solution)/shard_map/bij,bjk->bik/dot_general | solution.py:33
  37.9 1.0 fusion.21
  38.9 1.2 fusion.19
  40.1 1.0 copy-done.2
  41.7 1.9 %fusion.26 = f32[2,256,256]{2,1,0:T(8,128)S(1)} fusion(f32[4,256,256]{2,1,0:T(8,128)} %copy-done.2), kind=kOutput, calls=%fused_computation.32 | convolution fusion | flops 402653184 | bytes 1572864 | tf_op jit(solution)/shard_map/bij,bjk->bik/dot_general | solution.py:33
  44.3 43.9 %while.21 = (s32[]{:T(128)}, f32[256]{0:T(256)S(1)}, f32[256,256]{1,0:T(8,128)S(1)}, f32[256]{0:T(256)S(1)}, s32[]{:T(128)}) while((s32[]{:T(128)}, f32[256]{0:T(256)S(1)}, f32[256,256]{1,0:T(8,128)S(1)}, f32[256]{0:T(256)S(1)}, s32[]{:T(128)}) %tuple.61), condition=%wide.region_2.0_spmd, body=%wide.region_1.0_spmd.sunk | while | flops 786690 | bytes 271461 | solution.py:63
  44.6 3.8 %collective-permute-start = (f32[256]{0:T(256)S(1)}, f32[256]{0:T(256)S(1)}, u32[]{:S(2)}, u32[]{:S(2)}) collective-permute-start(f32[256]{0:T(256)S(1)} %add.329), channel_id=1, source_target_pairs={{0,4},{4,8},{8,12},{12,16},{16,20},{20,24},{24,28},{1,5},{5,9},{9,... | collective-permute-start | bytes 3080 | tf_op jit(solution)/shard_map/while/body/eval_jaxpr/ppermute | solution.py:17
  48.4 1.3 collective-permute-done
  50.0 4.2 %collective-permute-start = (f32[256]{0:T(256)S(1)}, f32[256]{0:T(256)S(1)}, u32[]{:S(2)}, u32[]{:S(2)}) collective-permute-start(f32[256]{0:T(256)S(1)} %add.329), channel_id=1, source_target_pairs={{0,4},{4,8},{8,12},{12,16},{16,20},{20,24},{24,28},{1,5},{5,9},{9,... | collective-permute-start | bytes 3080 | tf_op jit(solution)/shard_map/while/body/eval_jaxpr/ppermute | solution.py:17
  54.2 1.3 collective-permute-done
  55.7 4.4 %collective-permute-start = (f32[256]{0:T(256)S(1)}, f32[256]{0:T(256)S(1)}, u32[]{:S(2)}, u32[]{:S(2)}) collective-permute-start(f32[256]{0:T(256)S(1)} %add.329), channel_id=1, source_target_pairs={{0,4},{4,8},{8,12},{12,16},{16,20},{20,24},{24,28},{1,5},{5,9},{9,... | collective-permute-start | bytes 3080 | tf_op jit(solution)/shard_map/while/body/eval_jaxpr/ppermute | solution.py:17
  60.2 1.3 collective-permute-done
  61.7 5.1 %collective-permute-start = (f32[256]{0:T(256)S(1)}, f32[256]{0:T(256)S(1)}, u32[]{:S(2)}, u32[]{:S(2)}) collective-permute-start(f32[256]{0:T(256)S(1)} %add.329), channel_id=1, source_target_pairs={{0,4},{4,8},{8,12},{12,16},{16,20},{20,24},{24,28},{1,5},{5,9},{9,... | collective-permute-start | bytes 3080 | tf_op jit(solution)/shard_map/while/body/eval_jaxpr/ppermute | solution.py:17
  66.8 1.3 collective-permute-done
  68.4 5.1 %collective-permute-start = (f32[256]{0:T(256)S(1)}, f32[256]{0:T(256)S(1)}, u32[]{:S(2)}, u32[]{:S(2)}) collective-permute-start(f32[256]{0:T(256)S(1)} %add.329), channel_id=1, source_target_pairs={{0,4},{4,8},{8,12},{12,16},{16,20},{20,24},{24,28},{1,5},{5,9},{9,... | collective-permute-start | bytes 3080 | tf_op jit(solution)/shard_map/while/body/eval_jaxpr/ppermute | solution.py:17
  73.5 1.3 collective-permute-done
  75.1 5.1 %collective-permute-start = (f32[256]{0:T(256)S(1)}, f32[256]{0:T(256)S(1)}, u32[]{:S(2)}, u32[]{:S(2)}) collective-permute-start(f32[256]{0:T(256)S(1)} %add.329), channel_id=1, source_target_pairs={{0,4},{4,8},{8,12},{12,16},{16,20},{20,24},{24,28},{1,5},{5,9},{9,... | collective-permute-start | bytes 3080 | tf_op jit(solution)/shard_map/while/body/eval_jaxpr/ppermute | solution.py:17
  80.2 1.3 collective-permute-done
  81.8 5.1 %collective-permute-start = (f32[256]{0:T(256)S(1)}, f32[256]{0:T(256)S(1)}, u32[]{:S(2)}, u32[]{:S(2)}) collective-permute-start(f32[256]{0:T(256)S(1)} %add.329), channel_id=1, source_target_pairs={{0,4},{4,8},{8,12},{12,16},{16,20},{20,24},{24,28},{1,5},{5,9},{9,... | collective-permute-start | bytes 3080 | tf_op jit(solution)/shard_map/while/body/eval_jaxpr/ppermute | solution.py:17
  86.9 1.3 collective-permute-done
  88.6 1.6 %fusion.24 = f32[2,1,256]{2,1,0:T(1,128)S(1)} fusion(f32[4,256,256]{2,1,0:T(8,128)} %copy-done.2, f32[2,256,1]{1,0,2:T(2,128)S(1)} %get-tuple-element.101), kind=kOutput, calls=%fused_computation.30 | convolution fusion | flops 1572864 | bytes 528384 | tf_op jit(solution)/shard_map/bij,bj->bi/dot_general | solution.py:48
  90.2 1.0 fusion.17
  91.3 3.4 %fusion.8 = f32[8,1,256]{2,1,0:T(1,128)S(1)} fusion(f32[8,256,1]{1,2,0:T(1,128)S(1)} %reshape.99, f32[16,256,256]{2,1,0:T(8,128)} %copy-done.1), kind=kOutput, calls=%fused_computation.10 | convolution fusion | flops 6291456 | bytes 2113536 | tf_op jit(solution)/shard_map/bij,bj->bi/dot_general | solution.py:48
  94.8 5.8 %fusion = f32[16,1,256]{2,1,0:T(1,128)S(1)} fusion(f32[16,256,1]{1,2,0:T(1,128)S(1)} %reshape.101, f32[32,256,256]{2,1,0:T(8,128)} %broadcast_multiply_fusion), kind=kOutput, calls=%fused_computation.2 | convolution fusion | flops 12582912 | bytes 4227072 | tf_op jit(solution)/shard_map/bij,bj->bi/dot_general | solution.py:48
  100.8 7.6 %fusion.7 = f32[32,1,256]{2,1,0:T(1,128)S(1)} fusion(f32[32,256,1]{1,2,0:T(1,128)S(1)} %reshape.103, f32[256,256]{1,0:T(8,128)S(1)} %copy-done.4, f32[32,256]{1,0:T(8,128)S(1)} %get-tuple-element.76), kind=kOutput, calls=%fused_computation.9 | convolution fusion | flops 27262976 | bytes 360448 | tf_op jit(solution)/shard_map/tij,tj->ti/dot_general | solution.py:92
  110.4 45.1 %while.22 = (s32[]{:T(128)}, f32[256]{0:T(256)S(1)}, f32[256]{0:T(256)S(1)}, f32[256]{0:T(256)S(1)}, s32[]{:T(128)}) while((s32[]{:T(128)}, f32[256]{0:T(256)S(1)}, f32[256]{0:T(256)S(1)}, f32[256]{0:T(256)S(1)}, s32[]{:T(128)}) %tuple.63), condition=%wide.region_4.5_spmd, body=%wide.region_3.4_spmd.sunk | while | flops 514 | bytes 8293 | solution.py:73
  110.4 1.3 collective-permute-start.1
  111.7 5.3 %collective-permute-done.1 = f32[256]{0:T(256)S(1)} collective-permute-done((f32[256]{0:T(256)S(1)}, f32[256]{0:T(256)S(1)}, u32[]{:S(2)}, u32[]{:S(2)}) %collective-permute-start.1) | collective-permute-done | bytes 1056 | tf_op jit(solution)/shard_map/while/body/eval_jaxpr/ppermute | solution.py:17
  117.0 1.3 collective-permute-start.1
  118.3 5.3 %collective-permute-done.1 = f32[256]{0:T(256)S(1)} collective-permute-done((f32[256]{0:T(256)S(1)}, f32[256]{0:T(256)S(1)}, u32[]{:S(2)}, u32[]{:S(2)}) %collective-permute-start.1) | collective-permute-done | bytes 1056 | tf_op jit(solution)/shard_map/while/body/eval_jaxpr/ppermute | solution.py:17
  123.6 1.3 collective-permute-start.1
  124.9 5.1 %collective-permute-done.1 = f32[256]{0:T(256)S(1)} collective-permute-done((f32[256]{0:T(256)S(1)}, f32[256]{0:T(256)S(1)}, u32[]{:S(2)}, u32[]{:S(2)}) %collective-permute-start.1) | collective-permute-done | bytes 1056 | tf_op jit(solution)/shard_map/while/body/eval_jaxpr/ppermute | solution.py:17
  130.0 1.3 collective-permute-start.1
  131.3 5.1 %collective-permute-done.1 = f32[256]{0:T(256)S(1)} collective-permute-done((f32[256]{0:T(256)S(1)}, f32[256]{0:T(256)S(1)}, u32[]{:S(2)}, u32[]{:S(2)}) %collective-permute-start.1) | collective-permute-done | bytes 1056 | tf_op jit(solution)/shard_map/while/body/eval_jaxpr/ppermute | solution.py:17
  136.4 1.3 collective-permute-start.1
  137.6 5.1 %collective-permute-done.1 = f32[256]{0:T(256)S(1)} collective-permute-done((f32[256]{0:T(256)S(1)}, f32[256]{0:T(256)S(1)}, u32[]{:S(2)}, u32[]{:S(2)}) %collective-permute-start.1) | collective-permute-done | bytes 1056 | tf_op jit(solution)/shard_map/while/body/eval_jaxpr/ppermute | solution.py:17
  142.7 1.3 collective-permute-start.1
  144.0 5.1 %collective-permute-done.1 = f32[256]{0:T(256)S(1)} collective-permute-done((f32[256]{0:T(256)S(1)}, f32[256]{0:T(256)S(1)}, u32[]{:S(2)}, u32[]{:S(2)}) %collective-permute-start.1) | collective-permute-done | bytes 1056 | tf_op jit(solution)/shard_map/while/body/eval_jaxpr/ppermute | solution.py:17
  149.1 1.3 collective-permute-start.1
  150.4 5.1 %collective-permute-done.1 = f32[256]{0:T(256)S(1)} collective-permute-done((f32[256]{0:T(256)S(1)}, f32[256]{0:T(256)S(1)}, u32[]{:S(2)}, u32[]{:S(2)}) %collective-permute-start.1) | collective-permute-done | bytes 1056 | tf_op jit(solution)/shard_map/while/body/eval_jaxpr/ppermute | solution.py:17
  (156 shorter events, 6.5 us)
Async XLA Ops:
  0.6 1.1 copy-start
  0.6 10.8 %copy-start.6 = (f32[256]{0:T(256)S(1)}, f32[256]{0:T(256)}, u32[]{:S(2)}) copy-start(f32[256]{0:T(256)} %param.18) | copy-start | bytes 3076
  0.7 10.8 %copy-start.5 = (f32[32,256]{1,0:T(8,128)S(1)}, f32[32,256]{1,0:T(8,128)}, u32[]{:S(2)}) copy-start(f32[32,256]{1,0:T(8,128)} %param.20) | copy-start | bytes 98308
  0.7 10.8 %copy-start.3 = (f32[256,256]{1,0:T(8,128)S(1)}, f32[256,256]{1,0:T(8,128)}, u32[]{:S(2)}) copy-start(f32[256,256]{1,0:T(8,128)} %param.19) | copy-start | bytes 786436
  29.7 2.0 %copy-start.1 = (f32[16,256,256]{2,1,0:T(8,128)}, f32[16,256,256]{2,1,0:T(8,128)S(1)}, u32[]{:S(2)}) copy-start(f32[16,256,256]{2,1,0:T(8,128)S(1)} %fusion.2) | copy-start | bytes 12582916
  40.1 1.0 copy-start.2
  44.6 5.1 %collective-permute-start = (f32[256]{0:T(256)S(1)}, f32[256]{0:T(256)S(1)}, u32[]{:S(2)}, u32[]{:S(2)}) collective-permute-start(f32[256]{0:T(256)S(1)} %add.329), channel_id=1, source_target_pairs={{0,4},{4,8},{8,12},{12,16},{16,20},{20,24},{24,28},{1,5},{5,9},{9,... | collective-permute-start | bytes 3080 | tf_op jit(solution)/shard_map/while/body/eval_jaxpr/ppermute | solution.py:17
  50.0 5.5 %collective-permute-start = (f32[256]{0:T(256)S(1)}, f32[256]{0:T(256)S(1)}, u32[]{:S(2)}, u32[]{:S(2)}) collective-permute-start(f32[256]{0:T(256)S(1)} %add.329), channel_id=1, source_target_pairs={{0,4},{4,8},{8,12},{12,16},{16,20},{20,24},{24,28},{1,5},{5,9},{9,... | collective-permute-start | bytes 3080 | tf_op jit(solution)/shard_map/while/body/eval_jaxpr/ppermute | solution.py:17
  55.7 5.7 %collective-permute-start = (f32[256]{0:T(256)S(1)}, f32[256]{0:T(256)S(1)}, u32[]{:S(2)}, u32[]{:S(2)}) collective-permute-start(f32[256]{0:T(256)S(1)} %add.329), channel_id=1, source_target_pairs={{0,4},{4,8},{8,12},{12,16},{16,20},{20,24},{24,28},{1,5},{5,9},{9,... | collective-permute-start | bytes 3080 | tf_op jit(solution)/shard_map/while/body/eval_jaxpr/ppermute | solution.py:17
  61.7 6.4 %collective-permute-start = (f32[256]{0:T(256)S(1)}, f32[256]{0:T(256)S(1)}, u32[]{:S(2)}, u32[]{:S(2)}) collective-permute-start(f32[256]{0:T(256)S(1)} %add.329), channel_id=1, source_target_pairs={{0,4},{4,8},{8,12},{12,16},{16,20},{20,24},{24,28},{1,5},{5,9},{9,... | collective-permute-start | bytes 3080 | tf_op jit(solution)/shard_map/while/body/eval_jaxpr/ppermute | solution.py:17
  68.4 6.4 %collective-permute-start = (f32[256]{0:T(256)S(1)}, f32[256]{0:T(256)S(1)}, u32[]{:S(2)}, u32[]{:S(2)}) collective-permute-start(f32[256]{0:T(256)S(1)} %add.329), channel_id=1, source_target_pairs={{0,4},{4,8},{8,12},{12,16},{16,20},{20,24},{24,28},{1,5},{5,9},{9,... | collective-permute-start | bytes 3080 | tf_op jit(solution)/shard_map/while/body/eval_jaxpr/ppermute | solution.py:17
  75.1 6.4 %collective-permute-start = (f32[256]{0:T(256)S(1)}, f32[256]{0:T(256)S(1)}, u32[]{:S(2)}, u32[]{:S(2)}) collective-permute-start(f32[256]{0:T(256)S(1)} %add.329), channel_id=1, source_target_pairs={{0,4},{4,8},{8,12},{12,16},{16,20},{20,24},{24,28},{1,5},{5,9},{9,... | collective-permute-start | bytes 3080 | tf_op jit(solution)/shard_map/while/body/eval_jaxpr/ppermute | solution.py:17
  81.8 6.4 %collective-permute-start = (f32[256]{0:T(256)S(1)}, f32[256]{0:T(256)S(1)}, u32[]{:S(2)}, u32[]{:S(2)}) collective-permute-start(f32[256]{0:T(256)S(1)} %add.329), channel_id=1, source_target_pairs={{0,4},{4,8},{8,12},{12,16},{16,20},{20,24},{24,28},{1,5},{5,9},{9,... | collective-permute-start | bytes 3080 | tf_op jit(solution)/shard_map/while/body/eval_jaxpr/ppermute | solution.py:17
  88.5 12.2 %copy-start.4 = (f32[256,256]{1,0:T(8,128)S(1)}, f32[256,256]{1,0:T(8,128)}, u32[]{:S(2)}) copy-start(f32[256,256]{1,0:T(8,128)} %param.19) | copy-start | bytes 786436
  110.4 6.6 %collective-permute-start.1 = (f32[256]{0:T(256)S(1)}, f32[256]{0:T(256)S(1)}, u32[]{:S(2)}, u32[]{:S(2)}) collective-permute-start(f32[256]{0:T(256)S(1)} %multiply_add_fusion.7), channel_id=1, source_target_pairs={{4,0},{8,4},{12,8},{16,12},{20,16},{24,20},{28,24},{5,1},{9,5},{13... | collective-permute-start | bytes 3080 | tf_op jit(solution)/shard_map/while/body/eval_jaxpr/ppermute | solution.py:17
  117.0 6.6 %collective-permute-start.1 = (f32[256]{0:T(256)S(1)}, f32[256]{0:T(256)S(1)}, u32[]{:S(2)}, u32[]{:S(2)}) collective-permute-start(f32[256]{0:T(256)S(1)} %multiply_add_fusion.7), channel_id=1, source_target_pairs={{4,0},{8,4},{12,8},{16,12},{20,16},{24,20},{28,24},{5,1},{9,5},{13... | collective-permute-start | bytes 3080 | tf_op jit(solution)/shard_map/while/body/eval_jaxpr/ppermute | solution.py:17
  123.6 6.4 %collective-permute-start.1 = (f32[256]{0:T(256)S(1)}, f32[256]{0:T(256)S(1)}, u32[]{:S(2)}, u32[]{:S(2)}) collective-permute-start(f32[256]{0:T(256)S(1)} %multiply_add_fusion.7), channel_id=1, source_target_pairs={{4,0},{8,4},{12,8},{16,12},{20,16},{24,20},{28,24},{5,1},{9,5},{13... | collective-permute-start | bytes 3080 | tf_op jit(solution)/shard_map/while/body/eval_jaxpr/ppermute | solution.py:17
  130.0 6.4 %collective-permute-start.1 = (f32[256]{0:T(256)S(1)}, f32[256]{0:T(256)S(1)}, u32[]{:S(2)}, u32[]{:S(2)}) collective-permute-start(f32[256]{0:T(256)S(1)} %multiply_add_fusion.7), channel_id=1, source_target_pairs={{4,0},{8,4},{12,8},{16,12},{20,16},{24,20},{28,24},{5,1},{9,5},{13... | collective-permute-start | bytes 3080 | tf_op jit(solution)/shard_map/while/body/eval_jaxpr/ppermute | solution.py:17
  136.4 6.4 %collective-permute-start.1 = (f32[256]{0:T(256)S(1)}, f32[256]{0:T(256)S(1)}, u32[]{:S(2)}, u32[]{:S(2)}) collective-permute-start(f32[256]{0:T(256)S(1)} %multiply_add_fusion.7), channel_id=1, source_target_pairs={{4,0},{8,4},{12,8},{16,12},{20,16},{24,20},{28,24},{5,1},{9,5},{13... | collective-permute-start | bytes 3080 | tf_op jit(solution)/shard_map/while/body/eval_jaxpr/ppermute | solution.py:17
  142.7 6.4 %collective-permute-start.1 = (f32[256]{0:T(256)S(1)}, f32[256]{0:T(256)S(1)}, u32[]{:S(2)}, u32[]{:S(2)}) collective-permute-start(f32[256]{0:T(256)S(1)} %multiply_add_fusion.7), channel_id=1, source_target_pairs={{4,0},{8,4},{12,8},{16,12},{20,16},{24,20},{28,24},{5,1},{9,5},{13... | collective-permute-start | bytes 3080 | tf_op jit(solution)/shard_map/while/body/eval_jaxpr/ppermute | solution.py:17
  149.1 6.4 %collective-permute-start.1 = (f32[256]{0:T(256)S(1)}, f32[256]{0:T(256)S(1)}, u32[]{:S(2)}, u32[]{:S(2)}) collective-permute-start(f32[256]{0:T(256)S(1)} %multiply_add_fusion.7), channel_id=1, source_target_pairs={{4,0},{8,4},{12,8},{16,12},{20,16},{24,20},{28,24},{5,1},{9,5},{13... | collective-permute-start | bytes 3080 | tf_op jit(solution)/shard_map/while/body/eval_jaxpr/ppermute | solution.py:17
